TPU v7x, 32 devices: a whole 2x2x4 slice. The times are simulated.
32 devices in a mesh: tm: 4 (over y, x), sat: 8 (over z, core).
Axes of the slice: x: 2, y: 2, z: 4, core: 2. Of those that a mesh axis runs over, the one named last changes fastest.
Arguments:
- samples: int32 [2, 8, 8192], P(None, 'tm', 'sat'), may hold values from -1073741824 to 1073741823
- codes: int32 [24, 4092], P('sat'), may hold values from -1 to 1, as said below
- dopplers: int32 [16], replicated, may hold values from -60 to 60
Outputs:
- power: float32 [16, 24, 8192], P('tm', 'sat')
- detection: float32 [24], P('sat')
Inputs may be any that keep to these rules, and one draw needn't show every extreme that they name: `codes`: each entry is -1 or 1.
All inputs are finite; a program needn't handle non-finite values.
Results may differ from a plain program's by a relative error of at most 0.0003.
Values sent between devices are 32-bit elements.
A program may use at most 64 MiB of HBM per device.

v0:
```python
import math

import jax
import jax.numpy as jnp
from jax import lax
from jax.sharding import PartitionSpec as P

sample_scale = 2.0 ** (-29)
wrap_count = 32768


def dft_angles(outer, inner):
    sample_length = outer * inner
    rows_outer = jnp.arange(outer, dtype=jnp.int32)
    rows_inner = jnp.arange(inner, dtype=jnp.int32)
    angle_outer = jnp.mod(rows_outer[:, None] * rows_outer[None, :], outer).astype(jnp.float32) * (
        2.0 * math.pi / outer
    )
    angle_twist = jnp.mod(rows_outer[:, None] * rows_inner[None, :], sample_length).astype(
        jnp.float32
    ) * (2.0 * math.pi / sample_length)
    angle_inner = jnp.mod(rows_inner[:, None] * rows_inner[None, :], inner).astype(jnp.float32) * (
        2.0 * math.pi / inner
    )
    return (angle_outer, angle_twist, angle_inner)


def unit_pair(angles, direction):
    return (jnp.cos(angles), direction * jnp.sin(angles))


def product_complex(pattern, left_pair, right_pair):

    def contract(first_operand, right_term):
        return jnp.einsum(pattern, first_operand, right_term, precision=lax.Precision.HIGHEST)

    return (
        contract(left_pair[0], right_pair[0]) - contract(left_pair[1], right_pair[1]),
        contract(left_pair[0], right_pair[1]) + contract(left_pair[1], right_pair[0]),
    )


def twisted(pair, factor):
    return (pair[0] * factor[0] - pair[1] * factor[1], pair[0] * factor[1] + pair[1] * factor[0])


def forward_dft(pair):
    sample_length = pair[0].shape[-1]
    inner = min(128, sample_length)
    outer = sample_length // inner
    leading = pair[0].shape[:-1]
    shaped = (pair[0].reshape(leading + (outer, inner)), pair[1].reshape(leading + (outer, inner)))
    angle_outer, angle_twist, angle_inner = dft_angles(outer, inner)
    sectioned = product_complex("kn,...nm->...km", unit_pair(angle_outer, -1.0), shaped)
    sectioned = twisted(sectioned, unit_pair(angle_twist, -1.0))
    return product_complex("...kn,nm->...km", sectioned, unit_pair(angle_inner, -1.0))


def inverse_dft(pair):
    outer = pair[0].shape[-2]
    inner = pair[0].shape[-1]
    angle_outer, angle_twist, angle_inner = dft_angles(outer, inner)
    sectioned = product_complex("...kn,nm->...km", pair, unit_pair(angle_inner, 1.0))
    sectioned = twisted(sectioned, unit_pair(angle_twist, 1.0))
    return product_complex("nk,...km->...nm", unit_pair(angle_outer, 1.0), sectioned)


def replica_rows(code_rows, sample_length):
    chip_count = code_rows.shape[1]
    offsets = jnp.arange(sample_length, dtype=jnp.int32)
    chip_index = offsets * chip_count // sample_length
    halves = jnp.mod(offsets * (2 * chip_count) // sample_length, 2)
    sign_rows = (1 - 2 * halves).astype(jnp.float32)
    return jnp.take(code_rows, chip_index, axis=1).astype(jnp.float32) * sign_rows[None, :]


def to_float(block_ints):
    return (
        block_ints[0].astype(jnp.float32) * sample_scale,
        block_ints[1].astype(jnp.float32) * sample_scale,
    )


def block_powers(signal_pair, bin_rows, code_spectra):
    signal_real, signal_imag = signal_pair
    sample_length = signal_real.shape[-1]
    offsets = jnp.arange(sample_length, dtype=jnp.int32)
    rotation_angles = jnp.mod(bin_rows[:, None] * offsets[None, :], wrap_count).astype(
        jnp.float32
    ) * (2.0 * math.pi / wrap_count)
    cosine = jnp.cos(rotation_angles)[:, None, :]
    sine_part = jnp.sin(rotation_angles)[:, None, :]
    wiped_record = (
        signal_real[None] * cosine + signal_imag[None] * sine_part,
        signal_imag[None] * cosine - signal_real[None] * sine_part,
    )
    spectra = forward_dft(wiped_record)
    code_real = code_spectra[0][None, None]
    code_imag = code_spectra[1][None, None]
    spec_real = spectra[0][:, :, None]
    spec_imag = spectra[1][:, :, None]
    cross = (
        spec_real * code_real + spec_imag * code_imag,
        spec_imag * code_real - spec_real * code_imag,
    )
    lagged = inverse_dft(cross)
    powers = (lagged[0] * lagged[0] + lagged[1] * lagged[1]) * (1.0 / float(sample_length) ** 3)
    return powers.reshape(powers.shape[:3] + (sample_length,))


def shards(samples, codes, dopplers):
    sample_length = samples.shape[2] * lax.axis_size("sat")
    segment = samples.astype(jnp.float32) * sample_scale
    local_power = jnp.sum(segment * segment)
    own_blocks = lax.all_gather(samples, "sat", axis=2, tiled=True)
    replicas = replica_rows(codes, sample_length)
    code_spectra = forward_dft((replicas, jnp.zeros_like(replicas)))
    segment_tally = own_blocks.shape[1] * lax.axis_size("tm")
    dop_rows = dopplers.shape[0] // lax.axis_size("tm")
    own_pair = to_float(own_blocks)

    def one_group(cluster_frequencies):
        return jnp.sum(block_powers(own_pair, cluster_frequencies, code_spectra), axis=1)

    summed = lax.map(one_group, dopplers.reshape(-1, dop_rows))
    integrated = lax.psum_scatter(
        summed.reshape((dop_rows * lax.axis_size("tm"),) + summed.shape[2:]),
        "tm",
        scatter_dimension=0,
        tiled=True,
    )
    power_map = integrated * (1.0 / segment_tally)
    peak_local = jnp.max(power_map, axis=(0, 2))
    power_sum = lax.psum(local_power, ("tm", "sat"))
    peak_value = lax.pmax(peak_local, "tm")
    average_energy = power_sum / float(segment_tally * sample_length)
    detection = peak_value / jnp.maximum(average_energy, 0.25)
    return (power_map, detection)


def solution(mesh):
    placed = (P(None, "tm", "sat"), P("sat", None), P())
    return jax.shard_map(
        shards,
        mesh=mesh,
        in_specs=placed,
        out_specs=(P("tm", "sat", None), P("sat")),
        check_vma=False,
    )
```

profile of v0, /device:TPU:0, one launch (start us, length us, event | category | flops | bytes accessed | tf_op | source)
XLA Modules:
  0.0 199.9 jit_solution(15598807219510786838)
XLA Ops:
  8.0 1.5 copy.12
  9.5 27.7 %gather_fusion = s32[8192,3]{1,0:T(8,128)} fusion(s32[3,4092]{0,1:T(8,128)S(1)} %copy.12, s32[8192]{0:T(1024)S(1)} %broadcast_clamp_fusion), kind=kCustom, calls=%fused_computation | custom fusion | bytes 229376 | tf_op jit(solution)/shard_map/jit(_take)/gather | solution.py:74
  37.2 2.8 %copy.13 = s32[3,64,128]{2,1,0:T(8,128)S(1)} copy(s32[3,64,128]{0,2,1:T(8,128)} %bitcast.153) | data formatting | bytes 196608 | tf_op jit(solution)/shard_map/jit(_take)/gather | solution.py:74
  43.2 15.7 %all_gather.3 = s32[2,2,8192]{2,1,0:T(2,128)S(1)} all-gather(s32[2,2,1024]{2,1,0:T(2,128)S(1)} %copy-done), channel_id=1, replica_groups=mesh['tm'=4,'sat'=8] {'sat'}, dimensions={2}, use_global_device_ids=true | all-gather | bytes 147456 | tf_op jit(solution)/shard_map/all_gather | solution.py:115
  59.0 58.5 %while.13 = (s32[]{:T(128)}, f32[4,4,3,8192]{3,1,0,2:T(4,128)S(1)}, f32[2,8192]{1,0:T(2,128)S(1)}, s32[4,4]{1,0:T(4,128)S(1)}, f32[2,8192]{1,0:T(2,128)S(1)}, /*...) while((s32[]{:T(128)}, f32[4,4,3,8192]{3,1,0,2:T(4,128)S(1)}, f32[2,8192]{1,0:T(2,128)S(1)}, ...), condition=%wide.region_2.3_spmd, body=%wide.region_0.2_spmd.sunk | while | flops 2427191296 | bytes 28737676 | solution.py:125
  59.2 0.6 fusion.342
  62.2 0.6 fusion.348
  62.8 0.6 convolution_subtract_fusion.8
  63.5 0.6 fusion.347
  64.1 0.6 convolution_add_fusion.8
  64.7 1.0 fusion.350
  65.7 1.0 convolution_subtract_fusion.9
  66.8 1.0 fusion.349
  67.8 1.0 convolution_add_fusion.9
  69.0 1.1 fusion.354
  70.1 1.0 fusion.352
  71.1 1.0 fusion.353
  72.2 1.1 fusion.355
  73.8 0.6 fusion.342
  76.8 0.6 fusion.348
  77.4 0.6 convolution_subtract_fusion.8
  78.1 0.6 fusion.347
  78.7 0.6 convolution_add_fusion.8
  79.3 1.0 fusion.350
  80.3 1.0 convolution_subtract_fusion.9
  81.4 1.0 fusion.349
  82.4 1.0 convolution_add_fusion.9
  83.6 1.1 fusion.354
  84.6 1.0 fusion.352
  85.7 1.0 fusion.353
  86.8 1.1 fusion.355
  88.4 0.6 fusion.342
  91.4 0.6 fusion.348
  92.0 0.6 convolution_subtract_fusion.8
  92.6 0.6 fusion.347
  93.3 0.6 convolution_add_fusion.8
  93.9 1.0 fusion.350
  94.9 1.0 convolution_subtract_fusion.9
  96.0 1.0 fusion.349
  97.0 1.0 convolution_add_fusion.9
  98.2 1.1 fusion.354
  99.2 1.0 fusion.352
  100.3 1.0 fusion.353
  101.3 1.1 fusion.355
  103.0 0.6 fusion.342
  106.0 0.6 fusion.348
  106.6 0.6 convolution_subtract_fusion.8
  107.2 0.6 fusion.347
  107.9 0.6 convolution_add_fusion.8
  108.5 1.0 fusion.350
  109.5 1.0 convolution_subtract_fusion.9
  110.5 1.0 fusion.349
  111.6 1.0 convolution_add_fusion.9
  112.8 1.1 fusion.354
  113.8 1.0 fusion.352
  114.9 1.0 fusion.353
  115.9 1.1 fusion.355
  117.5 1.7 reshape.326
  119.2 0.6 multiply_reduce_fusion
  119.8 40.9 %psum.7 = f32[]{:T(128)} all-reduce(f32[]{:T(128)} %multiply_reduce_fusion), channel_id=1, replica_groups=mesh['tm'=4,'sat'=8] {'tm','sat'}, use_global_device_ids=true, to_apply=%region_7.8 | all-reduce | flops 1 | bytes 8 | tf_op jit(solution)/shard_map/psum | solution.py:134
  160.7 0.6 dynamic-slice
  162.6 19.0 %all-reduce.3.cloned.1.call-done = f32[16,3,8192]{2,0,1:T(8,128)} async-done(((f32[16,3,8192]{2,0,1:T(8,128)}), f32[16,3,8192]{2,0,1:T(8,128)}) %all-reduce.3.cloned.1.call-update) | async-done | bytes 1572880
  181.6 2.0 %fusion.295 = (f32[3]{0:T(128)S(1)}, f32[4,3,8192]{2,0,1:T(4,128)}) fusion(f32[16,3,8192]{2,0,1:T(8,128)} %all-reduce.3.cloned.1.call-done, u32[]{:T(128)S(6)} %multiply.11), kind=kLoop, calls=%fused_computation.354 | loop fusion | flops 196605 | bytes 786448 | tf_op jit(solution)/shard_map/reduce_max | solution.py:133
  183.6 8.9 %pmax.7 = f32[3]{0:T(128)S(1)} all-reduce(f32[3]{0:T(128)S(1)} %get-tuple-element.140), channel_id=1, replica_groups=mesh['tm'=4,'sat'=8] {'tm'}, use_global_device_ids=true, to_apply=%region_5.6 | all-reduce | flops 3 | bytes 24 | tf_op jit(solution)/shard_map/pmax | solution.py:135
  (69 shorter events, 16.5 us)
Async XLA Ops:
  7.2 174.5 %all-reduce.3.cloned.1.call-start = ((), (), s32[]{:S(2)}) async-start(), calls=%async_computation | async-start | bytes 3145728
  40.0 3.1 %copy-start = (s32[2,2,1024]{2,1,0:T(2,128)S(1)}, s32[2,2,1024]{2,1,0:T(2,128)}, u32[]{:S(2)}) copy-start(s32[2,2,1024]{2,1,0:T(2,128)} %param.5) | copy-start | bytes 49156
  40.0 18.9 %copy-start.1 = (s32[16]{0:T(128)S(1)}, s32[16]{0:T(128)}, u32[]{:S(2)}) copy-start(s32[16]{0:T(128)} %param.7) | copy-start | bytes 196
  119.2 41.5 %copy-start.2 = (u32[32]{0:T(128)S(1)}, u32[32]{0:T(128)}, u32[]{:S(2)}) copy-start(u32[32]{0:T(128)} %constant.275) | copy-start | bytes 388
Sparse Core Ops, SparseCore 0:
  119.4 62.2 all-reduce.2
where the time goes:
time: 200 us
  blocking collectives  65.5 us (33%)
  matrix products  55.5 us (28%)
  local copies, waits for them, and re-layouts  36.3 us (18%)
  waiting for transfers between devices  19 us (10%)
  between operations  15.5 us (8%)
  other arithmetic  7.21 us (4%)
    dot_general x72, matrix products, contract(): jnp.einsum(pattern, first_operand, right_term, precision=lax.Precision.HI...  55.5 us
    psum x1, blocking collectives, shards(): power_sum = lax.psum(local_power, ('tm', 'sat'))  40.9 us
    gather x2, local copies, waits for them, and re-layouts, replica_rows(): jnp.take(code_rows, chip_index, axis=1).astype(jnp.float32)  30.5 us
    unnamed x2, waiting for transfers between devices  19 us
    all_gather x1, blocking collectives, shards(): own_blocks = lax.all_gather(samples, 'sat', axis=2, tiled=True)  15.7 us
    pmax x1, blocking collectives, shards(): peak_value = lax.pmax(peak_local, 'tm')  8.9 us
  transfers between devices with their start and end apart: 1, of which 1 were waited for; matrix products, arithmetic and copies ran while one was open for 1% of the time, Pallas kernels for 0%

commit v1 on v0

v1 whole, which is shorter than its diff:
```python
import functools
import math

import jax
import jax.numpy as jnp
import ml_dtypes
import numpy as np
from jax import lax
from jax.experimental import pallas as pl
from jax.experimental.pallas import tpu as pltpu
from jax.sharding import PartitionSpec as P

sample_scale = 2.0 ** (-29)
wrap_count = 32768
LANES = 128


def halves(table):
    high = table.astype(np.float32).astype(ml_dtypes.bfloat16)
    low = (table - high.astype(np.float64)).astype(np.float32).astype(ml_dtypes.bfloat16)
    return high, low


@functools.lru_cache(maxsize=None)
def tables(sample_length, chip_count):
    inner = LANES
    outer = sample_length // inner
    a = np.arange(outer)
    c = np.arange(inner)
    ang_o = 2 * np.pi * (np.outer(a, a) % outer) / outer
    ang_t = 2 * np.pi * (np.outer(a, c) % sample_length) / sample_length
    ang_i = 2 * np.pi * (np.outer(c, c) % inner) / inner
    fc, fs = np.cos(ang_o), -np.sin(ang_o)
    first = np.block([[fc, -fs], [fs, fc]])
    second = np.block([[-fs, -fc], [fc, -fs]])
    wc, ws = np.cos(ang_i), -np.sin(ang_i)
    fh, fl = halves(np.block([[wc, ws], [-ws, wc]]))
    ih, il = halves(np.block([[wc, -ws], [ws, wc]]))
    bh, bl = halves(np.block([[fc, fs], [-fs, fc]]))
    ch, cl = halves(np.concatenate([fc, fs], axis=0))
    offsets = np.arange(sample_length).reshape(outer, inner)
    chips = offsets * chip_count // sample_length
    signs = 1 - 2 * ((offsets * 2 * chip_count // sample_length) % 2)
    starts = tuple(int(v) for v in chips[:, 0])
    within = chips - chips[:, :1]
    return dict(
        first=first.astype(np.float32),
        second=second.astype(np.float32),
        twist=np.stack([np.cos(ang_t), -np.sin(ang_t)]).astype(np.float32),
        fwd=np.concatenate([fh, fh, fl], axis=0),
        inv=np.concatenate([ih, ih, il], axis=0),
        back=np.concatenate([bh, bh, bl], axis=1),
        code=np.concatenate([ch, cl], axis=1),
        within=within.astype(np.int32),
        signs=signs.astype(np.float32),
    ), starts


NAMES = ("first", "second", "twist", "fwd", "inv", "back", "code", "within", "signs")


def split(value):
    high = value.astype(jnp.bfloat16)
    low = (value - high.astype(jnp.float32)).astype(jnp.bfloat16)
    return high, low


def mm(left, right):
    return jnp.dot(left, right, preferred_element_type=jnp.float32)


def kernel(starts, outer, chip_count, x_ref, codes_ref, dop_ref, first_ref, second_ref, twist_ref,
           fwd_ref, inv_ref, back_ref, code_ref, within_ref, signs_ref,
           power_ref, peak_ref, cpad, gath, cspec, rot, dtw, energy):
    inner = LANES
    tm_count, sat_count, _, own, rows, _ = x_ref.shape
    blocks = tm_count * own
    dop_rows, sats = power_ref.shape[0], power_ref.shape[1]
    sample_length = outer * inner

    cpad[...] = jnp.zeros_like(cpad)
    cpad[0:sats, 0:chip_count] = codes_ref[...].astype(jnp.float32)
    for n1 in range(outer):
        base = starts[n1] // LANES * LANES
        shift = starts[n1] - base
        piece = cpad[:, base:base + 2 * LANES]
        if shift:
            piece = pltpu.roll(piece, 2 * LANES - shift, 1)
        for s in range(sats):
            gath[s, n1:n1 + 1, :] = piece[s:s + 1, :LANES]
    scale = math.sqrt(1.0 / (float(sample_length) ** 3 * blocks))
    t_re, t_im = twist_ref[0], twist_ref[1]
    for s in range(sats):
        rep = jnp.take_along_axis(gath[s], within_ref[...], axis=1) * signs_ref[...]
        rep = rep.astype(jnp.bfloat16)
        y = mm(code_ref[...], jnp.concatenate([rep, rep], axis=0))
        y_re, y_im = y[:outer], y[outer:]
        z = jnp.concatenate([y_re * t_re - y_im * t_im, y_re * t_im + y_im * t_re], axis=1)
        zh, zl = split(z)
        cspec[s] = mm(jnp.concatenate([zh, zl, zh], axis=1), fwd_ref[...]) * scale

    col = lax.broadcasted_iota(jnp.int32, (8, inner), 1)
    row_of = lax.rem(col, outer) * inner
    base_row = lax.axis_index("tm") * dop_rows
    for f in range(dop_rows):
        d = dop_ref[base_row + f]
        turn = 2.0 * math.pi / wrap_count
        a1 = ((row_of * d) & (wrap_count - 1)).astype(jnp.float32) * turn
        a2 = ((col * d) & (wrap_count - 1)).astype(jnp.float32) * turn
        c1, s1 = jnp.cos(a1)[0:1], -jnp.sin(a1)[0:1]
        c2, s2 = jnp.cos(a2)[0:1], -jnp.sin(a2)[0:1]
        mh, ml = split(first_ref[...] * c1 + second_ref[...] * s1)
        rot[f] = jnp.concatenate([mh, mh, ml], axis=1)
        dtw[f, 0] = t_re * c2 - t_im * s2
        dtw[f, 1] = t_re * s2 + t_im * c2

    energy[...] = jnp.zeros_like(energy)
    power_ref[...] = jnp.zeros_like(power_ref)

    def pair(g, carry):
        cols = []
        for blk in range(own):
            parts = [x_ref[g, q, part, blk] for part in range(2) for q in range(sat_count)]
            cols.append(jnp.concatenate(parts, axis=0))
        x = jnp.concatenate(cols, axis=1).astype(jnp.float32) * sample_scale
        sq = x * x
        energy[...] += jnp.sum(sq.reshape(2 * outer // 8, 8, own * inner), axis=0)
        xh, xl = split(x)
        xs = jnp.concatenate([xh, xl, xh], axis=0)
        for f in range(dop_rows):
            y = mm(rot[f], xs)
            u_re, u_im = dtw[f, 0], dtw[f, 1]
            zs = []
            for blk in range(own):
                y_re = y[:outer, blk * inner:(blk + 1) * inner]
                y_im = y[outer:, blk * inner:(blk + 1) * inner]
                zs.append(jnp.concatenate([y_re * u_re - y_im * u_im, y_re * u_im + y_im * u_re], axis=1))
            zh, zl = split(jnp.concatenate(zs, axis=0))
            spec = mm(jnp.concatenate([zh, zl, zh], axis=1), fwd_ref[...])
            crosses = []
            for s in range(sats):
                k_re, k_im = cspec[s, :, :inner], cspec[s, :, inner:]
                for blk in range(own):
                    s_re = spec[blk * outer:(blk + 1) * outer, :inner]
                    s_im = spec[blk * outer:(blk + 1) * outer, inner:]
                    crosses.append(jnp.concatenate(
                        [s_re * k_re + s_im * k_im, s_im * k_re - s_re * k_im], axis=1))
            ch, cl = split(jnp.concatenate(crosses, axis=0))
            lag = mm(jnp.concatenate([ch, cl, ch], axis=1), inv_ref[...])
            for s in range(sats):
                cols = []
                for blk in range(own):
                    at = (s * own + blk) * outer
                    l_re, l_im = lag[at:at + outer, :inner], lag[at:at + outer, inner:]
                    cols.append(jnp.concatenate(
                        [l_re * t_re + l_im * t_im, l_im * t_re - l_re * t_im], axis=0))
                wh, wl = split(jnp.concatenate(cols, axis=1))
                out = mm(back_ref[...], jnp.concatenate([wh, wl, wh], axis=0))
                o_re, o_im = out[:outer], out[outer:]
                p = o_re * o_re + o_im * o_im
                total = p[:, :inner]
                for blk in range(1, own):
                    total = total + p[:, blk * inner:(blk + 1) * inner]
                power_ref[f, s] += total
        return carry

    lax.fori_loop(0, tm_count, pair, 0)
    mean = jnp.sum(energy[...]) * (1.0 / float(blocks * sample_length))
    floor = jnp.maximum(mean, 0.25)
    for s in range(sats):
        top = power_ref[0, s]
        for f in range(1, dop_rows):
            top = jnp.maximum(top, power_ref[f, s])
        peak_ref[s:s + 1, :] = jnp.full((1, LANES), jnp.max(top), jnp.float32) / floor


def shards(samples, codes, dopplers):
    tm_count, sat_count = lax.axis_size("tm"), lax.axis_size("sat")
    own, segment = samples.shape[1], samples.shape[2]
    sample_length = segment * sat_count
    outer, rows = sample_length // LANES, segment // LANES
    sats, chip_count = codes.shape
    dop_rows = dopplers.shape[0] // tm_count
    consts, starts = tables(sample_length, chip_count)
    local = samples.reshape(2, own, rows, LANES)
    whole = lax.all_gather(local, ("tm", "sat"), axis=0)
    whole = whole.reshape(tm_count, sat_count, 2, own, rows, LANES)
    pad = (max(starts) // LANES + 2) * LANES
    pad = max(pad, -(-chip_count // LANES) * LANES)
    vm = pl.BlockSpec(memory_space=pltpu.VMEM)
    power, peak = pl.pallas_call(
        functools.partial(kernel, starts, outer, chip_count),
        out_shape=(
            jax.ShapeDtypeStruct((dop_rows, sats, outer, LANES), jnp.float32),
            jax.ShapeDtypeStruct((sats, LANES), jnp.float32),
        ),
        in_specs=[vm, vm, pl.BlockSpec(memory_space=pltpu.SMEM)] + [vm] * len(NAMES),
        out_specs=(vm, vm),
        scratch_shapes=[
            pltpu.VMEM((8, pad), jnp.float32),
            pltpu.VMEM((sats, outer, LANES), jnp.float32),
            pltpu.VMEM((sats, outer, 2 * LANES), jnp.float32),
            pltpu.VMEM((dop_rows, 2 * outer, 6 * outer), jnp.bfloat16),
            pltpu.VMEM((dop_rows, 2, outer, LANES), jnp.float32),
            pltpu.VMEM((8, own * LANES), jnp.float32),
        ],
        compiler_params=pltpu.CompilerParams(vmem_limit_bytes=48 * 1024 * 1024),
        name="search",
    )(whole, codes, dopplers, *[jnp.asarray(consts[n]) for n in NAMES])
    detection = lax.pmax(peak[:, 0], "tm")
    return power.reshape(dop_rows, sats, sample_length), detection


def solution(mesh):
    placed = (P(None, "tm", "sat"), P("sat", None), P())
    return jax.shard_map(
        shards,
        mesh=mesh,
        in_specs=placed,
        out_specs=(P("tm", "sat", None), P("sat")),
        check_vma=False,
    )
```

time: 200 us -> 80 us (0.40)
  matrix products: 55.5 us -> 0 us
  local copies, waits for them, and re-layouts: 36.3 us -> 7.52 us
  waiting for transfers between devices: 19 us -> 0 us
  Pallas kernels: 0 us -> 17.8 us
  between operations: 15.5 us -> 0.7 us
  blocking collectives: 65.5 us -> 53.5 us
  other arithmetic: 7.21 us -> 0 us
    dot_general x72 -> x0, matrix products: 55.5 us -> none  [contract(): jnp.einsum(pattern, first_operand, right_term, precision=lax.Precision.HI...]
    psum x1 -> x0, blocking collectives: 40.9 us -> none  [shards(): power_sum = lax.psum(local_power, ('tm', 'sat'))]
    gather x2 -> x0, local copies, waits for them, and re-layouts: 30.5 us -> none  [replica_rows(): jnp.take(code_rows, chip_index, axis=1).astype(jnp.float32)]
    all_gather x1, blocking collectives: 15.7 us -> 45.5 us  [shards(): whole = lax.all_gather(local, ('tm', 'sat'), axis=0)]
    unnamed x2 -> x0, waiting for transfers between devices: 19 us -> none
    pallas_call x0 -> x1, Pallas kernels: none -> 17.8 us  [shards(): pl.pallas_call(functools.partial(kernel, starts, outer, chip_count), out_...]
    unnamed x8 -> x22, local copies, waits for them, and re-layouts: 2.07 us -> 5.69 us
    cos x4 -> x0, other arithmetic: 2.37 us -> none  [block_powers(): cosine = jnp.cos(rotation_angles)[:, None, :]]
  transfers between devices with their start and end apart: 1 -> 0, of which waited for: 1 -> 0; matrix products, arithmetic and copies ran while one was open for 1% -> 0% of each run, Pallas kernels for 0% -> 0%
where the time goes in v1:
time: 80 us; the launch traced here: 79.5 us
  blocking collectives  53.5 us (67%)
  Pallas kernels  17.8 us (22%)
  local copies, waits for them, and re-layouts  7.52 us (9%)
    all_gather x1, blocking collectives, shards(): whole = lax.all_gather(local, ('tm', 'sat'), axis=0)  45.5 us
    pallas_call x1, Pallas kernels, shards(): pl.pallas_call(functools.partial(kernel, starts, outer, chip_count), out_...  17.8 us
    pmax x1, blocking collectives, shards(): detection = lax.pmax(peak[:, 0], 'tm')  7.97 us
    unnamed x22, local copies, waits for them, and re-layouts  5.69 us

profile of v1, /device:TPU:0, one launch (start us, length us, event | category | flops | bytes accessed | tf_op | source)
XLA Modules:
  0.0 79.5 jit_solution(7121377006196774819)
XLA Ops:
  0.6 0.0 copy-start.7
  0.6 0.0 copy-start
  0.7 0.8 all_gather_reshape.3
  1.4 0.0 copy-start.2
  1.5 0.0 copy-start.3
  1.5 45.5 %all_gather.3 = s32[32,2,2,8,128]{4,3,2,1,0:T(8,128)S(1)} all-gather(s32[1,2,2,8,128]{4,3,2,1,0:T(8,128)S(1)} %all_gather_reshape.3), channel_id=1, replica_groups=mesh['tm'=4,'sat'=8] {'tm','sat'}, dimensions={0}, use_global_device_ids=true | all-gather | bytes 540672 | tf_op jit(solution)/shard_map/all_gather | solution.py:186
  47.0 0.0 copy-start.10
  47.0 0.0 copy-done.7
  47.0 0.0 copy-done
  47.0 0.0 copy-done.2
  47.0 0.0 copy-done.3
  47.0 0.6 copy-done.10
  47.6 0.0 copy-start.1
  47.6 1.0 %copy-done.1 = bf16[768,256]{1,0:T(8,128)(2,1)S(1)} copy-done((bf16[768,256]{1,0:T(8,128)(2,1)S(1)}, bf16[768,256]{1,0:T(8,128)(2,1)}, u32[]{:S(2)}) %copy-start.1) | copy-done | bytes 393240
  48.6 0.0 copy-start.4
  48.6 0.8 %copy-done.4 = f32[2,64,128]{2,1,0:T(8,128)S(1)} copy-done((f32[2,64,128]{2,1,0:T(8,128)S(1)}, f32[2,64,128]{2,1,0:T(8,128)}, u32[]{:S(2)}) %copy-start.4) | copy-done | bytes 65560
  49.5 0.0 copy-start.5
  49.5 0.8 %copy-done.5 = f32[128,128]{1,0:T(8,128)S(1)} copy-done((f32[128,128]{1,0:T(8,128)S(1)}, f32[128,128]{1,0:T(8,128)}, u32[]{:S(2)}) %copy-start.5) | copy-done | bytes 65560
  50.3 0.0 copy-start.6
  50.3 0.8 %copy-done.6 = f32[128,128]{1,0:T(8,128)S(1)} copy-done((f32[128,128]{1,0:T(8,128)S(1)}, f32[128,128]{1,0:T(8,128)}, u32[]{:S(2)}) %copy-start.6) | copy-done | bytes 65560
  51.2 0.0 copy-start.8
  51.2 0.8 copy-done.8
  51.9 0.0 copy-start.9
  51.9 0.8 copy-done.9
  52.7 17.8 %search.1 = (f32[4,3,64,128]{3,2,1,0:T(8,128)S(1)}, f32[3,128]{1,0:T(4,128)S(1)}) custom-call(s32[4,8,2,2,8,128]{5,4,3,2,1,0:T(8,128)S(1)} %bitcast.5, s32[3,4092]{1,0:T(4,128)S(1)} %copy-done.3, s32[16]{0:T(128)S(1)} %copy-done.10, f32[128,128]{1,0:T(8,128)S(1)} %copy-done.6, f32[128,128]{1,0:T(8,128)S(1)} %copy-done.5, f32[2,64,128]{2,1,0:T(8,128)S(1)} %copy-done.4, ...), custom_call_target="tpu_custom_call" | custom-call | tf_op jit(solution)/shard_map/search/pallas_call | solution.py:191
  70.5 0.9 %reshape.11 = f32[4,3,8192]{2,0,1:T(4,128)} reshape(f32[4,3,64,128]{3,2,0,1:T(8,128)S(1)} %copy.16) | data formatting | bytes 786432 | tf_op jit(solution)/shard_map/reshape | solution.py:211
  71.4 0.1 slice_reduce_fusion
  71.5 8.0 %pmax.7 = f32[3]{0:T(128)} all-reduce(f32[3]{0:T(128)S(1)} %slice_reduce_fusion), channel_id=1, replica_groups=mesh['tm'=4,'sat'=8] {'tm'}, use_global_device_ids=true, to_apply=%region_0.0 | all-reduce | flops 3 | bytes 24 | tf_op jit(solution)/shard_map/pmax | solution.py:210
  (1 shorter events, 0.0 us)
Async XLA Ops:
  0.6 46.4 %copy-start.7 = (f32[64,128]{1,0:T(8,128)S(1)}, f32[64,128]{1,0:T(8,128)}, u32[]{:S(2)}) copy-start(f32[64,128]{1,0:T(8,128)} %constant.26.clone.signs_ref) | copy-start | bytes 98308
  0.6 46.3 %copy-start = (bf16[768,256]{1,0:T(8,128)(2,1)S(1)}, bf16[768,256]{1,0:T(8,128)(2,1)}, u32[]{:S(2)}) copy-start(bf16[768,256]{1,0:T(8,128)(2,1)} %constant.22.clone.inv_ref) | copy-start | bytes 1179652
  1.4 45.5 %copy-start.2 = (bf16[128,384]{1,0:T(8,128)(2,1)S(1)}, bf16[128,384]{1,0:T(8,128)(2,1)}, u32[]{:S(2)}) copy-start(bf16[128,384]{1,0:T(8,128)(2,1)} %constant.23.clone.back_ref) | copy-start | bytes 294916
  1.5 45.5 %copy-start.3 = (s32[3,4092]{1,0:T(4,128)S(1)}, s32[3,4092]{1,0:T(4,128)}, u32[]{:S(2)}) copy-start(s32[3,4092]{1,0:T(4,128)} %codes_ref.1) | copy-start | bytes 147316
  47.0 0.7 copy-start.10
  47.6 1.0 %copy-start.1 = (bf16[768,256]{1,0:T(8,128)(2,1)S(1)}, bf16[768,256]{1,0:T(8,128)(2,1)}, u32[]{:S(2)}) copy-start(bf16[768,256]{1,0:T(8,128)(2,1)} %constant.21.clone.fwd_ref) | copy-start | bytes 1179652
  48.6 0.8 %copy-start.4 = (f32[2,64,128]{2,1,0:T(8,128)S(1)}, f32[2,64,128]{2,1,0:T(8,128)}, u32[]{:S(2)}) copy-start(f32[2,64,128]{2,1,0:T(8,128)} %constant.20.clone.twist_ref) | copy-start | bytes 196612
  49.5 0.8 %copy-start.5 = (f32[128,128]{1,0:T(8,128)S(1)}, f32[128,128]{1,0:T(8,128)}, u32[]{:S(2)}) copy-start(f32[128,128]{1,0:T(8,128)} %constant.19.clone.second_ref) | copy-start | bytes 196612
  50.3 0.8 %copy-start.6 = (f32[128,128]{1,0:T(8,128)S(1)}, f32[128,128]{1,0:T(8,128)}, u32[]{:S(2)}) copy-start(f32[128,128]{1,0:T(8,128)} %constant.18.clone.first_ref) | copy-start | bytes 196612
  51.2 0.8 copy-start.8
  51.9 0.8 copy-start.9

commit v2 on v1

--- a/solution.py
+++ b/solution.py
@@ -13,6 +13,7 @@
 sample_scale = 2.0 ** (-29)
 wrap_count = 32768
 LANES = 128
+MESH = pl.DeviceIdType.MESH
 
 
 def halves(table):
@@ -69,14 +70,38 @@
     return jnp.dot(left, right, preferred_element_type=jnp.float32)
 
 
-def kernel(starts, outer, chip_count, x_ref, codes_ref, dop_ref, first_ref, second_ref, twist_ref,
-           fwd_ref, inv_ref, back_ref, code_ref, within_ref, signs_ref,
-           power_ref, peak_ref, cpad, gath, cspec, rot, dtw, energy):
+def kernel(starts, outer, chip_count, x_ref, codes_ref, dop_ref, *refs):
+    count = len(NAMES)
+    hbm, refs = refs[:count], refs[count:]
+    power_ref, peak_ref = refs[:2]
+    tabs, refs = refs[2:2 + count], refs[2 + count:]
+    (everyone, cpad, gath, cspec, rot, dtw, energy, acc, peaks, mine,
+     tab_sem, own_sem, send1, recv1, send2, recv2, send3, recv3) = refs
+    first_ref, second_ref, twist_ref, fwd_ref, inv_ref, back_ref, code_ref, within_ref, signs_ref = tabs
     inner = LANES
-    tm_count, sat_count, _, own, rows, _ = x_ref.shape
+    tm_count, sat_count, _, own, rows, _ = everyone.shape
     blocks = tm_count * own
-    dop_rows, sats = power_ref.shape[0], power_ref.shape[1]
+    dop_rows, sats = acc.shape[0], acc.shape[1]
     sample_length = outer * inner
+    me_tm, me_sat = lax.axis_index("tm"), lax.axis_index("sat")
+
+    def tm_peer(k):
+        return lax.rem(me_tm + k, tm_count)
+
+    def sat_peer(k):
+        return lax.rem(me_sat + k, sat_count)
+
+    barrier = pltpu.get_barrier_semaphore()
+    for k in range(1, sat_count):
+        pl.semaphore_signal(barrier, inc=1, device_id={"sat": sat_peer(k)}, device_id_type=MESH)
+    for k in range(1, tm_count):
+        pl.semaphore_signal(barrier, inc=1, device_id={"tm": tm_peer(k)}, device_id_type=MESH)
+
+    loads = [pltpu.make_async_copy(h, t, tab_sem.at[i]) for i, (h, t) in enumerate(zip(hbm, tabs))]
+    for load in loads:
+        load.start()
+    place = pltpu.make_async_copy(x_ref, everyone.at[me_tm, me_sat], own_sem)
+    place.start()
 
     cpad[...] = jnp.zeros_like(cpad)
     cpad[0:sats, 0:chip_count] = codes_ref[...].astype(jnp.float32)
@@ -88,6 +113,41 @@
             piece = pltpu.roll(piece, 2 * LANES - shift, 1)
         for s in range(sats):
             gath[s, n1:n1 + 1, :] = piece[s:s + 1, :LANES]
+
+    pl.semaphore_wait(barrier, sat_count + tm_count - 2)
+
+    def along_sat(k):
+        return pltpu.make_async_remote_copy(
+            src_ref=x_ref, dst_ref=everyone.at[me_tm, me_sat], send_sem=send1.at[k - 1],
+            recv_sem=recv1.at[k - 1], device_id={"sat": sat_peer(k)}, device_id_type=MESH)
+
+    def from_sat(k):
+        src = sat_peer(sat_count - k)
+        return pltpu.make_async_remote_copy(
+            src_ref=x_ref, dst_ref=everyone.at[me_tm, src], send_sem=send1.at[k - 1],
+            recv_sem=recv1.at[k - 1], device_id={"sat": src}, device_id_type=MESH)
+
+    def along_tm(k):
+        return pltpu.make_async_remote_copy(
+            src_ref=everyone.at[me_tm], dst_ref=everyone.at[me_tm], send_sem=send2.at[k - 1],
+            recv_sem=recv2.at[k - 1], device_id={"tm": tm_peer(k)}, device_id_type=MESH)
+
+    def from_tm(k):
+        src = tm_peer(tm_count - k)
+        return pltpu.make_async_remote_copy(
+            src_ref=everyone.at[me_tm], dst_ref=everyone.at[src], send_sem=send2.at[k - 1],
+            recv_sem=recv2.at[k - 1], device_id={"tm": src}, device_id_type=MESH)
+
+    def share_peak(k):
+        return pltpu.make_async_remote_copy(
+            src_ref=mine, dst_ref=peaks.at[k - 1], send_sem=send3.at[k - 1],
+            recv_sem=recv3.at[k - 1], device_id={"tm": tm_peer(k)}, device_id_type=MESH)
+
+    for k in range(1, sat_count):
+        along_sat(k).start()
+    for load in loads:
+        load.wait()
+
     scale = math.sqrt(1.0 / (float(sample_length) ** 3 * blocks))
     t_re, t_im = twist_ref[0], twist_ref[1]
     for s in range(sats):
@@ -99,28 +159,44 @@
         zh, zl = split(z)
         cspec[s] = mm(jnp.concatenate([zh, zl, zh], axis=1), fwd_ref[...]) * scale
 
-    col = lax.broadcasted_iota(jnp.int32, (8, inner), 1)
-    row_of = lax.rem(col, outer) * inner
-    base_row = lax.axis_index("tm") * dop_rows
-    for f in range(dop_rows):
-        d = dop_ref[base_row + f]
-        turn = 2.0 * math.pi / wrap_count
-        a1 = ((row_of * d) & (wrap_count - 1)).astype(jnp.float32) * turn
-        a2 = ((col * d) & (wrap_count - 1)).astype(jnp.float32) * turn
-        c1, s1 = jnp.cos(a1)[0:1], -jnp.sin(a1)[0:1]
-        c2, s2 = jnp.cos(a2)[0:1], -jnp.sin(a2)[0:1]
-        mh, ml = split(first_ref[...] * c1 + second_ref[...] * s1)
-        rot[f] = jnp.concatenate([mh, mh, ml], axis=1)
-        dtw[f, 0] = t_re * c2 - t_im * s2
-        dtw[f, 1] = t_re * s2 + t_im * c2
+    lane = lax.broadcasted_iota(jnp.int32, (8, inner), 1)
+    row_of = lax.rem(lane, outer) * inner
+    base_row = me_tm * dop_rows
+    turn = 2.0 * math.pi / wrap_count
+    bins = lax.broadcasted_iota(jnp.int32, (8, inner), 0)
+    for f0 in range(0, dop_rows, 4):
+        d = jnp.zeros((8, inner), jnp.int32)
+        for f in range(f0, min(f0 + 4, dop_rows)):
+            d = jnp.where(lax.rem(bins, 4) == f - f0, dop_ref[base_row + f], d)
+        m = (jnp.where(bins < 4, row_of, lane) * d) & (wrap_count - 1)
+        angle = m.astype(jnp.float32) * turn
+        cosine, sine = jnp.cos(angle), -jnp.sin(angle)
+        for f in range(f0, min(f0 + 4, dop_rows)):
+            i = f - f0
+            c1, s1 = cosine[i:i + 1], sine[i:i + 1]
+            c2, s2 = cosine[i + 4:i + 5], sine[i + 4:i + 5]
+            mh, ml = split(first_ref[...] * c1 + second_ref[...] * s1)
+            rot[f] = jnp.concatenate([mh, mh, ml], axis=1)
+            dtw[f, 0] = t_re * c2 - t_im * s2
+            dtw[f, 1] = t_re * s2 + t_im * c2
 
     energy[...] = jnp.zeros_like(energy)
-    power_ref[...] = jnp.zeros_like(power_ref)
-
-    def pair(g, carry):
+    acc[...] = jnp.zeros_like(acc)
+    place.wait()
+    for k in range(1, sat_count):
+        from_sat(k).wait_recv()
+    for k in range(1, tm_count):
+        along_tm(k).start()
+
+    def group(j, carry):
+        @pl.when(j > 0)
+        def _():
+            from_tm(j).wait_recv()
+
+        g = tm_peer(tm_count - j)
         cols = []
         for blk in range(own):
-            parts = [x_ref[g, q, part, blk] for part in range(2) for q in range(sat_count)]
+            parts = [everyone[g, q, part, blk] for part in range(2) for q in range(sat_count)]
             cols.append(jnp.concatenate(parts, axis=0))
         x = jnp.concatenate(cols, axis=1).astype(jnp.float32) * sample_scale
         sq = x * x
@@ -161,17 +237,35 @@
                 total = p[:, :inner]
                 for blk in range(1, own):
                     total = total + p[:, blk * inner:(blk + 1) * inner]
-                power_ref[f, s] += total
+                acc[f, s] += total
         return carry
 
-    lax.fori_loop(0, tm_count, pair, 0)
+    lax.fori_loop(0, tm_count, group, 0)
+
+    mine[...] = jnp.zeros_like(mine)
+    for s in range(sats):
+        top = acc[0, s]
+        for f in range(1, dop_rows):
+            top = jnp.maximum(top, acc[f, s])
+        mine[s:s + 1, :] = jnp.max(top, axis=0, keepdims=True)
+    for k in range(1, sat_count):
+        along_sat(k).wait_send()
+    for k in range(1, tm_count):
+        along_tm(k).wait_send()
+    for f in range(dop_rows):
+        for s in range(sats):
+            power_ref[s, :, f, :] = acc[f, s]
+    for k in range(1, tm_count):
+        share_peak(k).start()
     mean = jnp.sum(energy[...]) * (1.0 / float(blocks * sample_length))
     floor = jnp.maximum(mean, 0.25)
-    for s in range(sats):
-        top = power_ref[0, s]
-        for f in range(1, dop_rows):
-            top = jnp.maximum(top, power_ref[f, s])
-        peak_ref[s:s + 1, :] = jnp.full((1, LANES), jnp.max(top), jnp.float32) / floor
+    for k in range(1, tm_count):
+        share_peak(k).wait()
+    best = mine[...]
+    for k in range(1, tm_count):
+        best = jnp.maximum(best, peaks[k - 1])
+    best = jnp.max(best, axis=1, keepdims=True)
+    peak_ref[...] = jnp.broadcast_to(best / floor, peak_ref.shape)
 
 
 def shards(samples, codes, dopplers):
@@ -183,32 +277,47 @@
     dop_rows = dopplers.shape[0] // tm_count
     consts, starts = tables(sample_length, chip_count)
     local = samples.reshape(2, own, rows, LANES)
-    whole = lax.all_gather(local, ("tm", "sat"), axis=0)
-    whole = whole.reshape(tm_count, sat_count, 2, own, rows, LANES)
     pad = (max(starts) // LANES + 2) * LANES
     pad = max(pad, -(-chip_count // LANES) * LANES)
+    peak_rows = -(-sats // 8) * 8
     vm = pl.BlockSpec(memory_space=pltpu.VMEM)
+    values = [jnp.asarray(consts[n]) for n in NAMES]
+    dma = pltpu.SemaphoreType.DMA
     power, peak = pl.pallas_call(
         functools.partial(kernel, starts, outer, chip_count),
         out_shape=(
-            jax.ShapeDtypeStruct((dop_rows, sats, outer, LANES), jnp.float32),
-            jax.ShapeDtypeStruct((sats, LANES), jnp.float32),
+            jax.ShapeDtypeStruct((sats, outer, dop_rows, LANES), jnp.float32),
+            jax.ShapeDtypeStruct((peak_rows, LANES), jnp.float32),
         ),
-        in_specs=[vm, vm, pl.BlockSpec(memory_space=pltpu.SMEM)] + [vm] * len(NAMES),
+        in_specs=[vm, vm, pl.BlockSpec(memory_space=pltpu.SMEM)]
+        + [pl.BlockSpec(memory_space=pltpu.HBM)] * len(NAMES),
         out_specs=(vm, vm),
-        scratch_shapes=[
+        scratch_shapes=[pltpu.VMEM(v.shape, v.dtype) for v in values] + [
+            pltpu.VMEM((tm_count, sat_count) + local.shape, jnp.int32),
             pltpu.VMEM((8, pad), jnp.float32),
             pltpu.VMEM((sats, outer, LANES), jnp.float32),
             pltpu.VMEM((sats, outer, 2 * LANES), jnp.float32),
             pltpu.VMEM((dop_rows, 2 * outer, 6 * outer), jnp.bfloat16),
             pltpu.VMEM((dop_rows, 2, outer, LANES), jnp.float32),
             pltpu.VMEM((8, own * LANES), jnp.float32),
+            pltpu.VMEM((dop_rows, sats, outer, LANES), jnp.float32),
+            pltpu.VMEM((tm_count - 1, peak_rows, LANES), jnp.float32),
+            pltpu.VMEM((peak_rows, LANES), jnp.float32),
+            dma((len(NAMES),)),
+            dma,
+            dma((sat_count - 1,)),
+            dma((sat_count - 1,)),
+            dma((tm_count - 1,)),
+            dma((tm_count - 1,)),
+            dma((tm_count - 1,)),
+            dma((tm_count - 1,)),
         ],
-        compiler_params=pltpu.CompilerParams(vmem_limit_bytes=48 * 1024 * 1024),
+        compiler_params=pltpu.CompilerParams(
+            vmem_limit_bytes=66_500_000, collective_id=0, has_side_effects=True),
         name="search",
-    )(whole, codes, dopplers, *[jnp.asarray(consts[n]) for n in NAMES])
-    detection = lax.pmax(peak[:, 0], "tm")
-    return power.reshape(dop_rows, sats, sample_length), detection
+    )(local, codes, dopplers, *values)
+    power = power.transpose(2, 0, 1, 3).reshape(dop_rows, sats, sample_length)
+    return power, peak[:sats, 0]
 
 
 def solution(mesh):

time: 80 us -> 37.4 us (0.47)
  blocking collectives: 53.5 us -> 0 us
  Pallas kernels: 17.8 us -> 32 us
  local copies, waits for them, and re-layouts: 7.52 us -> 4.4 us
    all_gather x1 -> x0, blocking collectives: 45.5 us -> none  [shards(): whole = lax.all_gather(local, ('tm', 'sat'), axis=0)]
    pallas_call x1, Pallas kernels: 17.8 us -> 32 us  [shards(): pl.pallas_call(functools.partial(kernel, starts, outer, chip_count), out_...]
    pmax x1 -> x0, blocking collectives: 7.97 us -> none  [shards(): detection = lax.pmax(peak[:, 0], 'tm')]
    unnamed x22 -> x3, local copies, waits for them, and re-layouts: 5.69 us -> 2.43 us
where the time goes in v2:
time: 37.4 us; the launch traced here: 37.1 us
  Pallas kernels  32 us (86%)
  local copies, waits for them, and re-layouts  4.4 us (12%)
  between operations  0.65 us (2%)
    pallas_call x1, Pallas kernels, shards(): pl.pallas_call(functools.partial(kernel, starts, outer, chip_count), out_...  32 us
    unnamed x3, local copies, waits for them, and re-layouts  2.43 us
    reshape x1, local copies, waits for them, and re-layouts, shards(): local = samples.reshape(2, own, rows, LANES)  1.34 us

profile of v2, /device:TPU:0, one launch (start us, length us, event | category | flops | bytes accessed | tf_op | source)
XLA Modules:
  0.0 37.1 jit_solution(4911152995807168397)
XLA Ops:
  0.6 1.3 %reshape.10.x_ref = s32[2,2,8,128]{3,2,1,0:T(8,128)} reshape(s32[2,2,1024]{2,1,0:T(2,128)} %param.12) | data formatting | bytes 32768 | tf_op jit(solution)/shard_map/reshape | solution.py:279
  2.0 32.0 %search.1 = (f32[3,64,4,128]{3,2,1,0:T(4,128)}, f32[8,128]{1,0:T(8,128)}) custom-call(s32[2,2,8,128]{3,2,1,0:T(8,128)} %reshape.10.x_ref, s32[3,4092]{1,0:T(4,128)} %codes_ref.1, s32[16]{0:T(128)} %dop_ref.1, f32[128,128]{1,0:T(8,128)} %constant.18.clone.refs_0_, f32[128,128]{1,0:T(8,128)} %constant.19.clone.refs_1_, f32[2,64,128]{2,1,0:T(8,128)} %constant.20.clone.refs_2_, ...), custom_call_target="tpu_custom_call" | custom-call | tf_op jit(solution)/shard_map/search/pallas_call | solution.py:286
  34.0 0.0 copy-start
  34.0 0.7 %copy-done = f32[8,128]{1,0:T(8,128)S(1)} copy-done((f32[8,128]{1,0:T(8,128)S(1)}, f32[8,128]{1,0:T(8,128)}, u32[]{:S(2)}) %copy-start) | copy-done | bytes 4120
  34.7 0.6 %slice_reduce_fusion = f32[3]{0:T(128)} fusion(f32[8,128]{1,0:T(8,128)S(1)} %copy-done), kind=kLoop, calls=%fused_computation | loop fusion | bytes 24 | tf_op jit(solution)/shard_map/slice | solution.py:320
  35.3 1.8 %copy.15 = f32[4,3,8192]{2,0,1:T(4,128)} copy(f32[4,3,8192]{2,0,1:T(4,128)} %bitcast.3) | data formatting | bytes 786432
Async XLA Ops:
  34.0 0.7 %copy-start = (f32[8,128]{1,0:T(8,128)S(1)}, f32[8,128]{1,0:T(8,128)}, u32[]{:S(2)}) copy-start(f32[8,128]{1,0:T(8,128)} %get-tuple-element.5) | copy-start | bytes 12292

commit v3 on v2

--- a/solution.py
+++ b/solution.py
@@ -13,6 +13,8 @@
 sample_scale = 2.0 ** (-29)
 wrap_count = 32768
 LANES = 128
+KERNEL_BYTES = 65_900_000
+PADDING = 1_200_000
 MESH = pl.DeviceIdType.MESH
 
 
@@ -44,20 +46,16 @@
     signs = 1 - 2 * ((offsets * 2 * chip_count // sample_length) % 2)
     starts = tuple(int(v) for v in chips[:, 0])
     within = chips - chips[:, :1]
-    return dict(
-        first=first.astype(np.float32),
-        second=second.astype(np.float32),
-        twist=np.stack([np.cos(ang_t), -np.sin(ang_t)]).astype(np.float32),
-        fwd=np.concatenate([fh, fh, fl], axis=0),
-        inv=np.concatenate([ih, ih, il], axis=0),
-        back=np.concatenate([bh, bh, bl], axis=1),
-        code=np.concatenate([ch, cl], axis=1),
-        within=within.astype(np.int32),
-        signs=signs.astype(np.float32),
-    ), starts
-
-
-NAMES = ("first", "second", "twist", "fwd", "inv", "back", "code", "within", "signs")
+    wide = np.concatenate([fh, fh, fl, ih, ih, il], axis=0)
+    narrow = [first, second, np.cos(ang_t), -np.sin(ang_t), bh, bl,
+              np.concatenate([ch, cl], axis=1), within, signs]
+    narrow = np.concatenate([np.asarray(t, np.float32) for t in narrow], axis=0)
+    return wide, narrow, starts
+
+
+def padded(table, size):
+    extra = -(-size // (table.shape[1] * table.dtype.itemsize)) - table.shape[0]
+    return np.pad(table, ((0, max(extra, 0)), (0, 0)))
 
 
 def split(value):
@@ -70,41 +68,56 @@
     return jnp.dot(left, right, preferred_element_type=jnp.float32)
 
 
-def kernel(starts, outer, chip_count, x_ref, codes_ref, dop_ref, *refs):
-    count = len(NAMES)
-    hbm, refs = refs[:count], refs[count:]
-    power_ref, peak_ref = refs[:2]
-    tabs, refs = refs[2:2 + count], refs[2 + count:]
-    (everyone, cpad, gath, cspec, rot, dtw, energy, acc, peaks, mine,
-     tab_sem, own_sem, send1, recv1, send2, recv2, send3, recv3) = refs
-    first_ref, second_ref, twist_ref, fwd_ref, inv_ref, back_ref, code_ref, within_ref, signs_ref = tabs
+def kernel(starts, outer, chip_count, cores, x_ref, codes_ref, dop_ref, wide_hbm, narrow_hbm,
+           power_ref, peak_ref, raw, chips, wide, narrow, back,
+           everyone, cpad, gath, cspec, rot, dtw, energy, acc, peaks, mine,
+           tab_sem, send1, recv1, send2, recv2, send3, recv3, send4, recv4):
     inner = LANES
-    tm_count, sat_count, _, own, rows, _ = everyone.shape
+    tm_count, _, line, _, own, rows, _ = everyone.shape
+    sat_count = cores * line
     blocks = tm_count * own
     dop_rows, sats = acc.shape[0], acc.shape[1]
     sample_length = outer * inner
     me_tm, me_sat = lax.axis_index("tm"), lax.axis_index("sat")
+    me_z, me_core = me_sat // cores, lax.rem(me_sat, cores)
+    twin = me_z * cores + (cores - 1 - me_core)
 
     def tm_peer(k):
         return lax.rem(me_tm + k, tm_count)
 
-    def sat_peer(k):
-        return lax.rem(me_sat + k, sat_count)
+    def tm_source(k):
+        return lax.rem(me_tm + tm_count - k, tm_count)
+
+    def z_peer(k):
+        return lax.rem(me_z + k, line)
+
+    def z_source(k):
+        return lax.rem(me_z + line - k, line)
 
     barrier = pltpu.get_barrier_semaphore()
-    for k in range(1, sat_count):
-        pl.semaphore_signal(barrier, inc=1, device_id={"sat": sat_peer(k)}, device_id_type=MESH)
+    for k in range(1, line):
+        pl.semaphore_signal(barrier, inc=1, device_id={"sat": z_peer(k) * cores + me_core}, device_id_type=MESH)
     for k in range(1, tm_count):
         pl.semaphore_signal(barrier, inc=1, device_id={"tm": tm_peer(k)}, device_id_type=MESH)
-
-    loads = [pltpu.make_async_copy(h, t, tab_sem.at[i]) for i, (h, t) in enumerate(zip(hbm, tabs))]
+    if cores > 1:
+        pl.semaphore_signal(barrier, inc=1, device_id={"sat": twin}, device_id_type=MESH)
+
+    pairs = ((x_ref, raw), (codes_ref, chips),
+             (narrow_hbm.at[pl.ds(0, narrow.shape[0])], narrow),
+             (wide_hbm.at[pl.ds(0, wide.shape[0])], wide))
+    loads = [pltpu.make_async_copy(h, t, tab_sem.at[i]) for i, (h, t) in enumerate(pairs)]
     for load in loads:
         load.start()
-    place = pltpu.make_async_copy(x_ref, everyone.at[me_tm, me_sat], own_sem)
-    place.start()
+    loads[0].wait()
+    for part in range(2):
+        for r in range(rows):
+            piece = raw[part, :, r * LANES:(r + 1) * LANES]
+            for blk in range(own):
+                everyone[me_tm, me_core, me_z, part, blk, r:r + 1, :] = piece[blk:blk + 1]
+    loads[1].wait()
 
     cpad[...] = jnp.zeros_like(cpad)
-    cpad[0:sats, 0:chip_count] = codes_ref[...].astype(jnp.float32)
+    cpad[0:sats, 0:chip_count] = chips[...].astype(jnp.float32)
     for n1 in range(outer):
         base = starts[n1] // LANES * LANES
         shift = starts[n1] - base
@@ -114,46 +127,58 @@
         for s in range(sats):
             gath[s, n1:n1 + 1, :] = piece[s:s + 1, :LANES]
 
-    pl.semaphore_wait(barrier, sat_count + tm_count - 2)
-
-    def along_sat(k):
+    pl.semaphore_wait(barrier, line + tm_count + cores - 3)
+
+    def along_z(k, at):
         return pltpu.make_async_remote_copy(
-            src_ref=x_ref, dst_ref=everyone.at[me_tm, me_sat], send_sem=send1.at[k - 1],
-            recv_sem=recv1.at[k - 1], device_id={"sat": sat_peer(k)}, device_id_type=MESH)
-
-    def from_sat(k):
-        src = sat_peer(sat_count - k)
+            src_ref=everyone.at[me_tm, me_core, me_z], dst_ref=everyone.at[me_tm, me_core, at],
+            send_sem=send1.at[k - 1], recv_sem=recv1.at[k - 1],
+            device_id={"sat": z_peer(k) * cores + me_core}, device_id_type=MESH)
+
+    def along_tm(k, at):
         return pltpu.make_async_remote_copy(
-            src_ref=x_ref, dst_ref=everyone.at[me_tm, src], send_sem=send1.at[k - 1],
-            recv_sem=recv1.at[k - 1], device_id={"sat": src}, device_id_type=MESH)
-
-    def along_tm(k):
+            src_ref=everyone.at[me_tm, me_core], dst_ref=everyone.at[at, me_core],
+            send_sem=send2.at[k - 1], recv_sem=recv2.at[k - 1],
+            device_id={"tm": tm_peer(k)}, device_id_type=MESH)
+
+    def to_twin(k, at_core):
+        g = tm_source(k)
         return pltpu.make_async_remote_copy(
-            src_ref=everyone.at[me_tm], dst_ref=everyone.at[me_tm], send_sem=send2.at[k - 1],
-            recv_sem=recv2.at[k - 1], device_id={"tm": tm_peer(k)}, device_id_type=MESH)
-
-    def from_tm(k):
-        src = tm_peer(tm_count - k)
-        return pltpu.make_async_remote_copy(
-            src_ref=everyone.at[me_tm], dst_ref=everyone.at[src], send_sem=send2.at[k - 1],
-            recv_sem=recv2.at[k - 1], device_id={"tm": src}, device_id_type=MESH)
+            src_ref=everyone.at[g, me_core], dst_ref=everyone.at[g, at_core],
+            send_sem=send4.at[k], recv_sem=recv4.at[k],
+            device_id={"sat": twin}, device_id_type=MESH)
 
     def share_peak(k):
         return pltpu.make_async_remote_copy(
             src_ref=mine, dst_ref=peaks.at[k - 1], send_sem=send3.at[k - 1],
             recv_sem=recv3.at[k - 1], device_id={"tm": tm_peer(k)}, device_id_type=MESH)
 
-    for k in range(1, sat_count):
-        along_sat(k).start()
-    for load in loads:
-        load.wait()
-
+    for k in range(1, line):
+        along_z(k, me_z).start()
+    loads[2].wait()
+    loads[3].wait()
+
+    cut = [0]
+
+    def take(count):
+        cut.append(cut[-1] + count)
+        return narrow[cut[-2]:cut[-1]]
+
+    first, second = take(2 * outer), take(2 * outer)
+    t_re, t_im = take(outer), take(outer)
+    bh, bl = take(2 * outer).astype(jnp.bfloat16), take(2 * outer).astype(jnp.bfloat16)
+    back[...] = jnp.concatenate([bh, bh, bl], axis=1)
+    code = take(2 * outer).astype(jnp.bfloat16)
+    within = take(outer).astype(jnp.int32)
+    signs = take(outer)
+    t_at = 4 * outer
+    fwd_ref = wide.at[pl.ds(0, 6 * inner)]
+    inv_ref = wide.at[pl.ds(6 * inner, 6 * inner)]
     scale = math.sqrt(1.0 / (float(sample_length) ** 3 * blocks))
-    t_re, t_im = twist_ref[0], twist_ref[1]
     for s in range(sats):
-        rep = jnp.take_along_axis(gath[s], within_ref[...], axis=1) * signs_ref[...]
+        rep = jnp.take_along_axis(gath[s], within, axis=1) * signs
         rep = rep.astype(jnp.bfloat16)
-        y = mm(code_ref[...], jnp.concatenate([rep, rep], axis=0))
+        y = mm(code, jnp.concatenate([rep, rep], axis=0))
         y_re, y_im = y[:outer], y[outer:]
         z = jnp.concatenate([y_re * t_re - y_im * t_im, y_re * t_im + y_im * t_re], axis=1)
         zh, zl = split(z)
@@ -175,28 +200,40 @@
             i = f - f0
             c1, s1 = cosine[i:i + 1], sine[i:i + 1]
             c2, s2 = cosine[i + 4:i + 5], sine[i + 4:i + 5]
-            mh, ml = split(first_ref[...] * c1 + second_ref[...] * s1)
+            mh, ml = split(first * c1 + second * s1)
             rot[f] = jnp.concatenate([mh, mh, ml], axis=1)
             dtw[f, 0] = t_re * c2 - t_im * s2
             dtw[f, 1] = t_re * s2 + t_im * c2
 
     energy[...] = jnp.zeros_like(energy)
     acc[...] = jnp.zeros_like(acc)
-    place.wait()
-    for k in range(1, sat_count):
-        from_sat(k).wait_recv()
-    for k in range(1, tm_count):
-        along_tm(k).start()
+    for k in range(1, line):
+        along_z(k, z_source(k)).wait_recv()
+    for k in range(1, tm_count):
+        along_tm(k, me_tm).start()
+    if cores > 1:
+        to_twin(0, me_core).start()
 
     def group(j, carry):
-        @pl.when(j > 0)
+        @pl.when(j == 1)
         def _():
-            from_tm(j).wait_recv()
-
-        g = tm_peer(tm_count - j)
+            along_tm(j, tm_source(j)).wait_recv()
+            if cores > 1:
+                to_twin(j, me_core).start()
+
+        @pl.when((j > 0) & (j < tm_count - 1))
+        def _():
+            along_tm(j + 1, tm_source(j + 1)).wait_recv()
+            if cores > 1:
+                to_twin(j + 1, me_core).start()
+
+        if cores > 1:
+            to_twin(j, cores - 1 - me_core).wait_recv()
+        g = tm_source(j)
+        w_re, w_im = narrow[t_at:t_at + outer], narrow[t_at + outer:t_at + 2 * outer]
         cols = []
         for blk in range(own):
-            parts = [everyone[g, q, part, blk] for part in range(2) for q in range(sat_count)]
+            parts = [everyone[g, q % cores, q // cores, part, blk] for part in range(2) for q in range(sat_count)]
             cols.append(jnp.concatenate(parts, axis=0))
         x = jnp.concatenate(cols, axis=1).astype(jnp.float32) * sample_scale
         sq = x * x
@@ -229,9 +266,9 @@
                     at = (s * own + blk) * outer
                     l_re, l_im = lag[at:at + outer, :inner], lag[at:at + outer, inner:]
                     cols.append(jnp.concatenate(
-                        [l_re * t_re + l_im * t_im, l_im * t_re - l_re * t_im], axis=0))
+                        [l_re * w_re + l_im * w_im, l_im * w_re - l_re * w_im], axis=0))
                 wh, wl = split(jnp.concatenate(cols, axis=1))
-                out = mm(back_ref[...], jnp.concatenate([wh, wl, wh], axis=0))
+                out = mm(back[...], jnp.concatenate([wh, wl, wh], axis=0))
                 o_re, o_im = out[:outer], out[outer:]
                 p = o_re * o_re + o_im * o_im
                 total = p[:, :inner]
@@ -248,10 +285,13 @@
         for f in range(1, dop_rows):
             top = jnp.maximum(top, acc[f, s])
         mine[s:s + 1, :] = jnp.max(top, axis=0, keepdims=True)
-    for k in range(1, sat_count):
-        along_sat(k).wait_send()
-    for k in range(1, tm_count):
-        along_tm(k).wait_send()
+    for k in range(1, line):
+        along_z(k, me_z).wait_send()
+    for k in range(1, tm_count):
+        along_tm(k, me_tm).wait_send()
+    if cores > 1:
+        for k in range(tm_count):
+            to_twin(k, me_core).wait_send()
     for f in range(dop_rows):
         for s in range(sats):
             power_ref[s, :, f, :] = acc[f, s]
@@ -275,25 +315,30 @@
     outer, rows = sample_length // LANES, segment // LANES
     sats, chip_count = codes.shape
     dop_rows = dopplers.shape[0] // tm_count
-    consts, starts = tables(sample_length, chip_count)
-    local = samples.reshape(2, own, rows, LANES)
+    cores = 2 if sat_count % 2 == 0 else 1
+    line = sat_count // cores
+    wide, narrow, starts = tables(sample_length, chip_count)
     pad = (max(starts) // LANES + 2) * LANES
     pad = max(pad, -(-chip_count // LANES) * LANES)
     peak_rows = -(-sats // 8) * 8
     vm = pl.BlockSpec(memory_space=pltpu.VMEM)
-    values = [jnp.asarray(consts[n]) for n in NAMES]
+    hbm = pl.BlockSpec(memory_space=pltpu.HBM)
     dma = pltpu.SemaphoreType.DMA
     power, peak = pl.pallas_call(
-        functools.partial(kernel, starts, outer, chip_count),
+        functools.partial(kernel, starts, outer, chip_count, cores),
         out_shape=(
             jax.ShapeDtypeStruct((sats, outer, dop_rows, LANES), jnp.float32),
             jax.ShapeDtypeStruct((peak_rows, LANES), jnp.float32),
         ),
-        in_specs=[vm, vm, pl.BlockSpec(memory_space=pltpu.SMEM)]
-        + [pl.BlockSpec(memory_space=pltpu.HBM)] * len(NAMES),
+        in_specs=[hbm, hbm, pl.BlockSpec(memory_space=pltpu.SMEM), hbm, hbm],
         out_specs=(vm, vm),
-        scratch_shapes=[pltpu.VMEM(v.shape, v.dtype) for v in values] + [
-            pltpu.VMEM((tm_count, sat_count) + local.shape, jnp.int32),
+        scratch_shapes=[
+            pltpu.VMEM(samples.shape, jnp.int32),
+            pltpu.VMEM(codes.shape, jnp.int32),
+            pltpu.VMEM(wide.shape, jnp.bfloat16),
+            pltpu.VMEM(narrow.shape, jnp.float32),
+            pltpu.VMEM((2 * outer, 6 * outer), jnp.bfloat16),
+            pltpu.VMEM((tm_count, cores, line, 2, own, rows, LANES), jnp.int32),
             pltpu.VMEM((8, pad), jnp.float32),
             pltpu.VMEM((sats, outer, LANES), jnp.float32),
             pltpu.VMEM((sats, outer, 2 * LANES), jnp.float32),
@@ -303,19 +348,20 @@
             pltpu.VMEM((dop_rows, sats, outer, LANES), jnp.float32),
             pltpu.VMEM((tm_count - 1, peak_rows, LANES), jnp.float32),
             pltpu.VMEM((peak_rows, LANES), jnp.float32),
-            dma((len(NAMES),)),
-            dma,
-            dma((sat_count - 1,)),
-            dma((sat_count - 1,)),
+            dma((4,)),
+            dma((line - 1,)),
+            dma((line - 1,)),
             dma((tm_count - 1,)),
             dma((tm_count - 1,)),
             dma((tm_count - 1,)),
             dma((tm_count - 1,)),
+            dma((tm_count,)),
+            dma((tm_count,)),
         ],
         compiler_params=pltpu.CompilerParams(
-            vmem_limit_bytes=66_500_000, collective_id=0, has_side_effects=True),
+            vmem_limit_bytes=KERNEL_BYTES, collective_id=0, has_side_effects=True),
         name="search",
-    )(local, codes, dopplers, *values)
+    )(samples, codes, dopplers, jnp.asarray(padded(wide, PADDING)), jnp.asarray(padded(narrow, PADDING)))
     power = power.transpose(2, 0, 1, 3).reshape(dop_rows, sats, sample_length)
     return power, peak[:sats, 0]
 

time: 37.4 us -> 35.9 us (0.960)
  local copies, waits for them, and re-layouts: 4.4 us -> 3.07 us
    reshape x1 -> x0, local copies, waits for them, and re-layouts: 1.34 us -> none  [shards(): local = samples.reshape(2, own, rows, LANES)]
    slice x1, local copies, waits for them, and re-layouts: 0.63 us -> 1.3 us  [shards(): return (power, peak[:sats, 0])]
    unnamed x3 -> x1, local copies, waits for them, and re-layouts: 2.43 us -> 1.77 us
where the time goes in v3:
time: 35.9 us; the launch traced here: 35.6 us
  Pallas kernels  31.9 us (89%)
  local copies, waits for them, and re-layouts  3.07 us (9%)
  between operations  0.64 us (2%)
    pallas_call x1, Pallas kernels, shards(): pl.pallas_call(functools.partial(kernel, starts, outer, chip_count, cores...  31.9 us
    unnamed x1, local copies, waits for them, and re-layouts  1.77 us
    slice x1, local copies, waits for them, and re-layouts, shards(): return (power, peak[:sats, 0])  1.3 us

profile of v3, /device:TPU:0, one launch (start us, length us, event | category | flops | bytes accessed | tf_op | source)
XLA Modules:
  0.0 35.6 jit_solution(10012718346545966228)
XLA Ops:
  0.6 31.9 %search.1 = (f32[3,64,4,128]{3,2,1,0:T(4,128)}, f32[8,128]{1,0:T(8,128)}) custom-call(s32[2,2,1024]{2,1,0:T(2,128)} %x_ref.1, s32[3,4092]{1,0:T(4,128)} %codes_ref.1, s32[16]{0:T(128)} %dop_ref.1, bf16[2344,256]{1,0:T(8,128)(2,1)} %constant.4.clone.wide_hbm, f32[2344,128]{1,0:T(8,128)} %constant.5.clone.narrow_hbm), custom_call_target="tpu_custom_call" | custom-call | tf_op jit(solution)/shard_map/search/pallas_call | solution.py:327
  32.6 1.3 %slice_reduce_fusion = f32[3]{0:T(128)} fusion(f32[8,128]{1,0:T(8,128)} %get-tuple-element.5), kind=kLoop, calls=%fused_computation | loop fusion | bytes 24 | tf_op jit(solution)/shard_map/slice | solution.py:366
  33.9 1.8 %copy.8 = f32[4,3,8192]{2,0,1:T(4,128)} copy(f32[4,3,8192]{2,0,1:T(4,128)} %bitcast.3) | data formatting | bytes 786432

commit v4 on v3

--- a/solution.py
+++ b/solution.py
@@ -13,7 +13,7 @@
 sample_scale = 2.0 ** (-29)
 wrap_count = 32768
 LANES = 128
-KERNEL_BYTES = 65_900_000
+KERNEL_BYTES = 55_800_000
 PADDING = 1_200_000
 MESH = pl.DeviceIdType.MESH
 
@@ -82,11 +82,19 @@
     me_z, me_core = me_sat // cores, lax.rem(me_sat, cores)
     twin = me_z * cores + (cores - 1 - me_core)
 
+    paired = tm_count & (tm_count - 1) == 0
+
     def tm_peer(k):
-        return lax.rem(me_tm + k, tm_count)
+        if not paired:
+            return lax.rem(me_tm + k, tm_count)
+        peer, bit = 0, 1
+        while bit < tm_count:
+            peer = peer + ((me_tm // bit + k // bit) % 2) * bit
+            bit *= 2
+        return peer
 
     def tm_source(k):
-        return lax.rem(me_tm + tm_count - k, tm_count)
+        return tm_peer(k) if paired else lax.rem(me_tm + tm_count - k, tm_count)
 
     def z_peer(k):
         return lax.rem(me_z + k, line)

time: 35.9 us -> 35.5 us (0.989)
  Pallas kernels: 31.9 us -> 31 us
  local copies, waits for them, and re-layouts: 3.07 us -> 3.58 us
    unnamed x1 -> x7, local copies, waits for them, and re-layouts: 1.77 us -> 2.95 us
    pallas_call x1, Pallas kernels: 31.9 us -> 31 us  [shards(): pl.pallas_call(functools.partial(kernel, starts, outer, chip_count, cores...]
    slice x1, local copies, waits for them, and re-layouts: 1.3 us -> 0.63 us  [shards(): return (power, peak[:sats, 0])]
where the time goes in v4:
time: 35.5 us; the launch traced here: 35.2 us
  Pallas kernels  31 us (87%)
  local copies, waits for them, and re-layouts  3.58 us (10%)
  between operations  0.65 us (2%)
    pallas_call x1, Pallas kernels, shards(): pl.pallas_call(functools.partial(kernel, starts, outer, chip_count, cores...  31 us
    unnamed x7, local copies, waits for them, and re-layouts  2.95 us

profile of v4, /device:TPU:0, one launch (start us, length us, event | category | flops | bytes accessed | tf_op | source)
XLA Modules:
  0.0 35.2 jit_solution(1591641031031337676)
XLA Ops:
  0.6 0.0 copy-start
  0.6 0.8 %copy-done = s32[3,4092]{1,0:T(4,128)S(1)} copy-done((s32[3,4092]{1,0:T(4,128)S(1)}, s32[3,4092]{1,0:T(4,128)}, u32[]{:S(2)}) %copy-start) | copy-done | bytes 49128
  1.5 0.0 copy-start.1
  1.5 0.7 %copy-done.1 = s32[2,2,1024]{2,1,0:T(2,128)S(1)} copy-done((s32[2,2,1024]{2,1,0:T(2,128)S(1)}, s32[2,2,1024]{2,1,0:T(2,128)}, u32[]{:S(2)}) %copy-start.1) | copy-done | bytes 16408
  2.2 0.0 copy-start.2
  2.2 0.7 %copy-done.2 = s32[16]{0:T(128)S(1)} copy-done((s32[16]{0:T(128)S(1)}, s32[16]{0:T(128)}, u32[]{:S(2)}) %copy-start.2) | copy-done | bytes 88
  2.8 31.0 %search.1 = (f32[3,64,4,128]{3,2,1,0:T(4,128)S(1)}, f32[8,128]{1,0:T(8,128)S(1)}) custom-call(s32[2,2,1024]{2,1,0:T(2,128)S(1)} %copy-done.1, s32[3,4092]{1,0:T(4,128)S(1)} %copy-done, s32[16]{0:T(128)S(1)} %copy-done.2, bf16[2344,256]{1,0:T(8,128)(2,1)} %constant.4.clone.wide_hbm, f32[2344,128]{1,0:T(8,128)} %constant.5.clone.narrow_hbm), custom_call_target="tpu_custom_call" | custom-call | tf_op jit(solution)/shard_map/search/pallas_call | solution.py:335
  33.9 0.6 %slice_reduce_fusion = f32[3]{0:T(128)} fusion(f32[8,128]{1,0:T(8,128)S(1)} %get-tuple-element.5), kind=kLoop, calls=%fused_computation | loop fusion | bytes 24 | tf_op jit(solution)/shard_map/slice | solution.py:374
  34.5 0.7 %copy.8 = f32[4,3,8192]{2,0,1:T(4,128)} copy(f32[4,3,8192]{2,0,1:T(4,128)S(1)} %bitcast.3) | data formatting | bytes 786432
Async XLA Ops:
  0.6 0.8 %copy-start = (s32[3,4092]{1,0:T(4,128)S(1)}, s32[3,4092]{1,0:T(4,128)}, u32[]{:S(2)}) copy-start(s32[3,4092]{1,0:T(4,128)} %codes_ref.1) | copy-start | bytes 147316
  1.5 0.7 %copy-start.1 = (s32[2,2,1024]{2,1,0:T(2,128)S(1)}, s32[2,2,1024]{2,1,0:T(2,128)}, u32[]{:S(2)}) copy-start(s32[2,2,1024]{2,1,0:T(2,128)} %x_ref.1) | copy-start | bytes 49156
  2.2 0.7 %copy-start.2 = (s32[16]{0:T(128)S(1)}, s32[16]{0:T(128)}, u32[]{:S(2)}) copy-start(s32[16]{0:T(128)} %dop_ref.1) | copy-start | bytes 196
